TPU v7x, 32 devices: a whole 2x2x4 slice. The times are simulated.
32 devices in a mesh: groups: 2 (over y), gx: 4 (over z), gy: 4 (over x, core).
Axes of the slice: x: 2, y: 2, z: 4, core: 2. Of those that a mesh axis runs over, the one named last changes fastest.
Arguments:
- tokens: bfloat16 [2, 16, 16384], P(None, 'groups', 'gx'), parts along dimension 1, may hold values from -20 to 20, as said below
- lengths: int32 [2, 16], P(None, ('groups', 'gx')), parts along dimension 1, may hold values from 1 to 1024, as said below
- norm_gain: bfloat16 [16384], P('gx'), may hold values from 0.5 to 2
- w_query: bfloat16 [16384, 8192], P('gx', 'gy'), may hold values from -1.171875 to 1.171875
- key_value_weight: bfloat16 [16384, 4, 256], P('gx', 'gy'), may hold values from -0.046875 to 0.046875
- w_out: bfloat16 [8192, 16384], P('gy', 'gx'), may hold values from -0.0625 to 0.0625
- cache: bfloat16 [2, 16, 1024, 4, 2, 128], P(None, ('groups', 'gx'), None, 'gy'), parts along dimension 1, may hold values from -16 to 16
Outputs:
- layer_out: bfloat16 [2, 16, 16384], P(None, 'groups', 'gx'), parts along dimension 1
There are 2 independent parts, one for each index of `groups`. A program takes and returns all parts, laid end to end along the dimension named above; an argument that names none is the same for every part. Nothing has to cross between parts.
Inputs may be any that keep to these rules, and one draw needn't show every extreme that they name: `tokens`: entries vary with the feature and the row. `lengths`: some rollout has exactly 1024 cached positions in every draw.
All inputs are finite; a program needn't handle non-finite values.
Results may differ from a plain program's by a relative error of at most 0.012.
The roundings to bfloat16 on the way count: a program that leaves them out, or rounds other values in their place, can miss the bound.
Values may be sent and summed in bfloat16 or wider, within the bound.
A program may use at most 128 MiB of HBM per device.

v0:
```python
import jax
import jax.numpy as jnp
from jax import lax
from jax.sharding import PartitionSpec as P

MODEL_WIDTH = 16384
HEAD_SIZE = 128


def rotate(vectors, positions):
    half = vectors.shape[-1] // 2
    freq = 500000.0 ** (-2.0 * jnp.arange(half, dtype=jnp.float32) / vectors.shape[-1])
    angle = positions[..., None] * freq
    cosine = jnp.cos(angle)
    sine = jnp.sin(angle)
    first = vectors[..., :half]
    second = vectors[..., half:]
    return jnp.concatenate(
        [first * cosine - second * sine, second * cosine + first * sine], axis=-1
    )


def attend(query_sum, keyval_sum, local_squares, lengths, cache):
    batches, rows_here = lengths.shape
    score_scale = lax.rsqrt(local_squares / MODEL_WIDTH + 1e-05)
    heads_kv = keyval_sum.shape[2]
    query_group = query_sum.shape[2] // (heads_kv * HEAD_SIZE)
    query = (
        query_sum.reshape(batches, rows_here, heads_kv, query_group, HEAD_SIZE)
        * score_scale[:, :, None, None, None]
    )
    key_value = keyval_sum * score_scale[:, :, None, None]
    positions = lengths.astype(jnp.float32)
    rotated_query = rotate(query, positions[:, :, None, None]).astype(jnp.bfloat16)
    rkey = rotate(key_value[..., :HEAD_SIZE], positions[:, :, None])
    value_new = key_value[..., HEAD_SIZE:]
    inv_root = 1.0 / jnp.sqrt(jnp.float32(HEAD_SIZE))
    keys = cache[:, :, :, :, 0, :]
    values = cache[:, :, :, :, 1, :]
    scores = (
        jnp.einsum("mrkgd,mrskd->mrkgs", rotated_query, keys, preferred_element_type=jnp.float32)
        * inv_root
    )
    valid = jnp.arange(cache.shape[2], dtype=jnp.int32)[None, None, :] < lengths[:, :, None]
    scores = jnp.where(valid[:, :, None, None, :], scores, -1e30)
    new_score = (
        jnp.sum(rotated_query.astype(jnp.float32) * rkey[:, :, :, None, :], axis=-1) * inv_root
    )
    top = jnp.maximum(jnp.max(scores, axis=-1), new_score)
    weights = jnp.exp(scores - top[..., None])
    new_weight = jnp.exp(new_score - top)
    total = jnp.sum(weights, axis=-1) + new_weight
    summed = jnp.einsum(
        "mrkgs,mrskd->mrkgd",
        weights.astype(jnp.bfloat16),
        values,
        preferred_element_type=jnp.float32,
    )
    summed = summed + new_weight[..., None] * value_new[:, :, :, None, :]
    return (
        (summed / total[..., None])
        .astype(jnp.bfloat16)
        .reshape(batches, rows_here, heads_kv * query_group * HEAD_SIZE)
    )


def local(tokens, lengths, norm_gain, w_query, key_value_weight, w_out, cache):
    x_full = tokens.astype(jnp.float32)
    squares = jnp.sum(x_full * x_full, axis=-1)
    normed = (x_full * norm_gain.astype(jnp.float32)).astype(jnp.bfloat16)
    query_part = jnp.einsum("mrd,dc->mrc", normed, w_query, preferred_element_type=jnp.float32)
    keyval_part = jnp.einsum(
        "mrd,dkc->mrkc", normed, key_value_weight, preferred_element_type=jnp.float32
    )
    query_sum, keyval_sum, local_squares = (
        lax.psum_scatter(query_part, "gx", scatter_dimension=1, tiled=True),
        lax.psum_scatter(keyval_part, "gx", scatter_dimension=1, tiled=True),
        lax.psum_scatter(squares, "gx", scatter_dimension=1, tiled=True),
    )
    attended = attend(query_sum, keyval_sum, local_squares, lengths, cache)
    projected = jnp.einsum(
        "mrc,cd->mrd",
        lax.all_gather(attended, "gx", axis=1, tiled=True),
        w_out,
        preferred_element_type=jnp.float32,
    )
    summed_heads = lax.psum(projected, "gy")
    return (x_full + summed_heads).astype(jnp.bfloat16)


def solution(mesh):
    placed = (
        P(None, "groups", "gx"),
        P(None, ("groups", "gx")),
        P("gx"),
        P("gx", "gy"),
        P("gx", "gy", None),
        P("gy", "gx"),
        P(None, ("groups", "gx"), None, "gy", None, None),
    )
    return jax.shard_map(
        local, mesh=mesh, in_specs=placed, out_specs=P(None, "groups", "gx"), check_vma=False
    )
```

profile of v0, /device:TPU:0, one launch (start us, length us, event | category | flops | bytes accessed | tf_op | source)
XLA Modules:
  0.0 122.0 jit_solution(11372717634072038642)
XLA Ops:
  6.5 0.0 copy-start
  6.5 0.0 all-reduce.9.cloned.1.call-start
  6.5 0.8 convert_element_type.46
  7.4 0.0 copy-start.1
  7.4 0.0 copy-start.2
  7.4 8.8 %fusion.2 = f32[2,8,2048]{2,1,0:T(8,128)} fusion(bf16[4096,2048]{1,0:T(8,128)(2,1)} %param.10, bf16[2,8,4096]{2,1,0:T(8,128)(2,1)} %param.7, f32[4096]{0:T(1024)S(1)} %convert_element_type.46), kind=kOutput, calls=%fused_computation.2 | convolution fusion | flops 268632064 | bytes 17055744 | tf_op jit(solution)/shard_map/mrd,dc->mrc/dot_general | solution.py:71
  16.2 0.0 copy-start.3
  16.2 0.0 all-reduce.9.cloned.1.call-update
  16.2 0.0 all-reduce.7.cloned.1.call-start
  16.3 0.0 copy-done.1
  16.3 0.1 fusion.13
  16.4 0.0 copy-done.2
  16.4 0.1 iota_compare_fusion
  16.5 0.0 copy-done
  16.5 0.4 fusion.9
  16.9 0.0 copy-done.3
  16.9 0.7 dynamic-slice
  18.3 0.1 multiply_cosine_fusion.1
  18.4 20.8 %all-reduce.3 = (f32[2,8]{1,0:T(2,128)S(1)}, f32[2,8,1,256]{3,1,0,2:T(8,128)S(1)}) all-reduce(f32[2,8]{1,0:T(2,128)S(1)} %fusion.13, f32[2,8,1,256]{3,1,0,2:T(8,128)S(1)} %fusion.9), channel_id=3, replica_groups=mesh['groups'=2,'gx'=4,'gy'=4] {'gx'}, use_global_device_ids=true, to_apply=%region_2.0.clone | all-reduce | flops 4112 | bytes 32896
  39.2 0.1 fusion.32
  39.3 0.1 dynamic-slice_multiply_fusion
  39.4 0.1 fusion.29
  39.5 6.9 %fusion.35 = (bf16[2,2,1024,1,1,128]{5,4,3,2,1,0:T(2,128)(2,1)}, bf16[2,2,1024,1,1,128]{5,4,3,2,1,0:T(2,128)(2,1)}) fusion(bf16[2,2,1024,1,2,128]{5,4,3,2,1,0:T(2,128)(2,1)} %param.13), kind=kLoop, calls=%fused_computation.55 | loop fusion | bytes 4194304 | tf_op jit(solution)/shard_map/slice | solution.py:38
  46.4 0.1 maximum_bitcast_fusion
  46.5 7.3 %all-reduce.9.cloned.1.call-done = f32[2,8,2048]{2,1,0:T(8,128)} async-done(((f32[2,8,2048]{2,1,0:T(8,128)}), f32[2,8,2048]{2,1,0:T(8,128)}) %all-reduce.9.cloned.1.call-update) | async-done | bytes 131088
  53.9 0.9 constant_dynamic-slice_fusion
  54.8 0.1 broadcast_multiply_fusion
  54.9 0.1 subtract_convert_fusion
  55.0 0.2 multiply_reduce_fusion
  55.1 2.1 %fusion.36 = (f32[2,2,16]{2,1,0:T(2,128)S(1)}, f32[2,2,16,1024]{3,2,1,0:T(8,128)S(1)}) fusion(bf16[2,2,1024,1,1,128]{5,4,3,2,1,0:T(2,128)(2,1)} %get-tuple-element.9, bf16[2,2,16,64]{3,2,1,0:T(8,128)(2,1)S(1)} %bitcast.38, bf16[2,2,16,64]{3,2,1,0:T(8,128)(2,1)S(1)} %bitcast.37, pred[2,2,1024]{2,1,0:T(4,128)(4,1)S(1)} %iota_compare_fusion), kind=kOutput, calls=%fused_computation.56 | convolution fusion | flops 17006528 | bytes 1331456 | tf_op jit(solution)/shard_map/mrkgd,mrskd->mrkgs/dot_general | solution.py:41
  57.3 0.2 fusion.15
  57.5 1.9 %fusion.8 = bf16[2,2,16,128]{3,2,1,0:T(8,128)(2,1)S(1)} fusion(bf16[2,2,1024,1,1,128]{5,4,3,2,1,0:T(2,128)(2,1)} %get-tuple-element.10, f32[2,2,16,1024]{3,2,1,0:T(8,128)S(1)} %get-tuple-element.18, f32[2,2,16]{2,1,0:T(2,128)S(1)} %multiply_maximum_fusion, f32[2,2,16]{2,1,0:T(2,128)S(1)} %get-tuple-element.7, f32[2,2,128]{2,1,0:T(2,128)S(1)} %slice_bitcast_fusion, ...), kind=kOutput, calls=%fused_computation.10 | convolution fusion | flops 16941056 | bytes 1329920 | tf_op jit(solution)/shard_map/mrkgs,mrskd->mrkgd/dot_general | solution.py:53
  59.4 13.1 %all_gather.3 = bf16[2,8,2048]{2,0,1:T(2,128)(2,1)S(1)} all-gather(bf16[2,2,2048]{2,0,1:T(2,128)(2,1)S(1)} %copy.12), channel_id=1, replica_groups=mesh['groups'=2,'gx'=4,'gy'=4] {'gx'}, dimensions={1}, use_global_device_ids=true | all-gather | bytes 81920 | tf_op jit(solution)/shard_map/all_gather | solution.py:83
  72.6 8.8 %fusion = f32[2,8,4096]{2,1,0:T(8,128)} fusion(bf16[2048,4096]{1,0:T(8,128)(2,1)} %param.12, bf16[2,8,2048]{2,0,1:T(2,128)(2,1)S(1)} %all_gather.3), kind=kOutput, calls=%fused_computation | convolution fusion | flops 268435456 | bytes 17104896 | tf_op jit(solution)/shard_map/mrc,cd->mrd/dot_general | solution.py:81
  81.3 0.0 all-reduce.7.cloned.1.call-update
  81.3 32.2 %all-reduce.7.cloned.1.call-done = f32[2,8,4096]{2,1,0:T(8,128)} async-done(((f32[2,8,4096]{2,1,0:T(8,128)}), f32[2,8,4096]{2,1,0:T(8,128)}) %all-reduce.7.cloned.1.call-update) | async-done | bytes 262160 | tf_op jit(solution)/shard_map/psum | solution.py:87
  113.5 1.6 %fusion.14 = bf16[2,8,4096]{2,1,0:T(8,128)(2,1)} fusion(f32[2,8,4096]{2,1,0:T(8,128)} %all-reduce.7.cloned.1.call-done, bf16[2,8,4096]{2,1,0:T(8,128)(2,1)S(1)} %copy-done.1), kind=kLoop, calls=%fused_computation.19 | loop fusion | flops 196608 | bytes 524288 | tf_op jit(solution)/shard_map/convert_element_type | solution.py:88
  (8 shorter events, 0.1 us)
Async XLA Ops:
  6.5 10.0 %copy-start = (bf16[4096,1,256]{2,0,1:T(8,128)(2,1)S(1)}, bf16[4096,1,256]{2,0,1:T(8,128)(2,1)}, u32[]{:S(2)}) copy-start(bf16[4096,1,256]{2,0,1:T(8,128)(2,1)} %param.11) | copy-start | bytes 6291460
  6.5 47.3 %all-reduce.9.cloned.1.call-start = ((), (), s32[]{:S(2)}) async-start(), calls=%async_computation.1 | async-start | bytes 262144
  7.4 8.9 %copy-start.1 = (bf16[2,8,4096]{2,1,0:T(8,128)(2,1)S(1)}, bf16[2,8,4096]{2,1,0:T(8,128)(2,1)}, u32[]{:S(2)}) copy-start(bf16[2,8,4096]{2,1,0:T(8,128)(2,1)} %param.7) | copy-start | bytes 393220
  7.4 9.0 %copy-start.2 = (s32[2,2]{1,0:T(2,128)S(1)}, s32[2,2]{1,0:T(2,128)}, u32[]{:S(2)}) copy-start(s32[2,2]{1,0:T(2,128)} %param.8) | copy-start | bytes 52
  16.2 0.7 copy-start.3
  16.2 97.3 %all-reduce.7.cloned.1.call-start = ((), (), s32[]{:S(2)}) async-start(), calls=%async_computation | async-start | bytes 524288 | tf_op jit(solution)/shard_map/psum | solution.py:87
Sparse Core Ops, SparseCore 0:
  16.4 37.4 all-reduce.8
  81.5 31.9 all-reduce.6
where the time goes:
time: 122 us
  waiting for transfers between devices  39.5 us (32%)
  blocking collectives  33.9 us (28%)
  matrix products  22 us (18%)
  between operations  14.2 us (12%)
  local copies, waits for them, and re-layouts  8.61 us (7%)
  other arithmetic  3.71 us (3%)
    psum x1, waiting for transfers between devices, local(): summed_heads = lax.psum(projected, 'gy')  32.2 us
    unnamed x1, blocking collectives  20.8 us
    all_gather x1, blocking collectives, local(): lax.all_gather(attended, 'gx', axis=1, tiled=True)  13.1 us
    dot_general x1, matrix products, local(): jnp.einsum('mrd,dc->mrc', normed, w_query, preferred_element_type=jnp.flo...  8.81 us
    dot_general x1, matrix products, local(): jnp.einsum('mrc,cd->mrd', lax.all_gather(attended, 'gx', axis=1, tiled=Tr...  8.75 us
    unnamed x3, waiting for transfers between devices  7.38 us
    slice x1, local copies, waits for them, and re-layouts, attend(): keys = cache[:, :, :, :, 0, :]  6.95 us
  transfers between devices with their start and end apart: 2, of which 2 were waited for; matrix products, arithmetic and copies ran while one was open for 7% of the time, Pallas kernels for 0%

commit v1 on v0

v1 whole, which is shorter than its diff:
```python
import functools

import jax
import jax.numpy as jnp
import numpy as np
from jax import lax
from jax.experimental import pallas as pl
from jax.experimental.pallas import tpu as pltpu
from jax.sharding import PartitionSpec as P

MODEL_WIDTH = 16384
HEAD_SIZE = 128
ROPE_BASE = 500000.0
MESH = pl.DeviceIdType.MESH


def kernel(
    n, ny, q_chunk, o_chunk,
    lens, tok_hbm, gain_hbm, freq_hbm, wq_hbm, wk_hbm, wo_hbm, kv_hbm,
    out,
    tok, gain, freq, wq, wk, wo, kv, normed,
    send, recv, q_s, o_s, att_send, att_recv, x_s, ybuf, r1, s2, r2,
    small_sem, wq_sem, wk_sem, wo_sem, kv_sem,
    qs_sem, qr_sem, as_sem, ar_sem, d_send, d_recv, e_send, e_recv, f_send, f_recv,
):
    batches, rows, depth = tok.shape
    here = rows // n
    total_rows = batches * rows
    q_width = wq.shape[1]
    kv_width = wk.shape[1]
    heads = q_width // HEAD_SIZE
    out_width = wo.shape[1]
    nq = q_width // q_chunk
    no = out_width // o_chunk
    local_rows = batches * here
    positions = kv.shape[0] // local_rows
    half = total_rows // 2
    me = lax.axis_index("gx")
    my = lax.axis_index("gy")
    bit = lax.rem(my, 2)

    smalls = [
        pltpu.make_async_copy(tok_hbm, tok, small_sem.at[0]),
        pltpu.make_async_copy(gain_hbm, gain, small_sem.at[1]),
        pltpu.make_async_copy(freq_hbm, freq, small_sem.at[2]),
    ]
    for copy in smalls:
        copy.start()
    wk_copy = pltpu.make_async_copy(wk_hbm, wk, wk_sem)
    wk_copy.start()

    def wq_copy(c):
        cols = pl.ds(pl.multiple_of(c * q_chunk, q_chunk), q_chunk)
        return pltpu.make_async_copy(wq_hbm.at[:, cols], wq.at[:, cols], wq_sem.at[c])

    def wo_copy(c):
        cols = pl.ds(pl.multiple_of(c * o_chunk, o_chunk), o_chunk)
        return pltpu.make_async_copy(wo_hbm.at[:, cols], wo.at[:, cols], wo_sem.at[c])

    kv_copy = pltpu.make_async_copy(kv_hbm, kv, kv_sem)
    for c in range(nq):
        wq_copy(c).start()
    kv_copy.start()
    for c in range(no):
        wo_copy(c).start()

    barrier = pltpu.get_barrier_semaphore()

    def greet(d, carry):
        pl.semaphore_signal(
            barrier, inc=1, device_id={"gx": lax.rem(me + d, n)}, device_id_type=MESH
        )
        return carry

    lax.fori_loop(1, n, greet, 0)
    bits = ny.bit_length() - 1

    def across(level):
        step = 1 << level
        return my + step - 2 * step * lax.rem(my // step, 2)

    for level in range(bits):
        pl.semaphore_signal(barrier, inc=1, device_id={"gy": across(level)}, device_id_type=MESH)

    for copy in smalls:
        copy.wait()
    x = tok[...].astype(jnp.float32).reshape(total_rows, depth)
    normed[...] = (x * gain[...]).astype(jnp.bfloat16)
    squares = jnp.broadcast_to(jnp.sum(x * x, axis=1, keepdims=True), (total_rows, HEAD_SIZE))

    def put(part, start):
        width = part.shape[1]
        for j in range(n):
            for b in range(batches):
                send[j, b * here:(b + 1) * here, pl.ds(start, width)] = part[
                    b * rows + j * here:b * rows + (j + 1) * here, :
                ]

    def shift(c, d, start, width):
        target = lax.rem(me + d, n)
        cols = pl.ds(start, width)
        return pltpu.make_async_remote_copy(
            src_ref=send.at[target, :, cols],
            dst_ref=recv.at[me, :, cols],
            send_sem=qs_sem.at[c, d],
            recv_sem=qr_sem.at[c, d],
            device_id={"gx": target},
            device_id_type=MESH,
        )

    def arrive(c, d, start, width):
        source = lax.rem(me - d + n, n)
        cols = pl.ds(start, width)
        return pltpu.make_async_remote_copy(
            src_ref=send.at[source, :, cols],
            dst_ref=recv.at[source, :, cols],
            send_sem=qs_sem.at[c, d],
            recv_sem=qr_sem.at[c, d],
            device_id={"gx": source},
            device_id_type=MESH,
        )

    def each(fn):
        def body(d, carry):
            fn(d)
            return carry
        lax.fori_loop(1, n, body, 0)

    wk_copy.wait()
    xn = normed[...]
    put(jnp.dot(xn, wk[...], preferred_element_type=jnp.float32), q_width)
    put(squares, q_width + kv_width)
    pl.semaphore_wait(barrier, n - 1 + bits)
    side = kv_width + HEAD_SIZE
    each(lambda d: shift(nq, d, q_width, side).start())

    def project(c, carry):
        start = pl.multiple_of(c * q_chunk, q_chunk)
        wq_copy(c).wait()
        put(
            jnp.dot(
                normed[...], wq[:, pl.ds(start, q_chunk)], preferred_element_type=jnp.float32
            ),
            start,
        )
        each(lambda d: shift(c, d, start, q_chunk).start())
        return carry

    lax.fori_loop(0, nq, project, 0)

    lane = lax.broadcasted_iota(jnp.int32, (local_rows, HEAD_SIZE), 1)
    row = lax.broadcasted_iota(jnp.int32, (local_rows, HEAD_SIZE), 0)
    place = jnp.zeros((local_rows, HEAD_SIZE), jnp.float32)
    for r in range(local_rows):
        place = jnp.where(row == r, lens[r // here, r % here].astype(jnp.float32), place)
    angle = place * freq[...]
    cosine = jnp.cos(angle)
    sine = jnp.sin(angle)
    sine = jnp.where(lane < HEAD_SIZE // 2, -sine, sine)

    def rotate(v):
        return v * cosine + pltpu.roll(v, HEAD_SIZE // 2, 1) * sine

    def finish(c, start, width):
        each(lambda d: arrive(c, d, start, width).wait_recv())

    def summed(start, width):
        cols = pl.ds(start, width)
        total = send[me, :, cols]

        def add(d, acc):
            return acc + recv[lax.rem(me + d, n), :, cols]

        return lax.fori_loop(1, n, add, total, unroll=n <= 8)

    finish(nq, q_width, side)
    tail = summed(q_width, side)
    scale = lax.rsqrt(tail[:, kv_width:] / MODEL_WIDTH + 1e-05)
    rkey = rotate(tail[:, :HEAD_SIZE] * scale)
    value_new = tail[:, HEAD_SIZE:2 * HEAD_SIZE] * scale

    for c in range(nq):
        finish(c, c * q_chunk, q_chunk)
        block = summed(c * q_chunk, q_chunk)
        for h in range(q_chunk // HEAD_SIZE):
            q_s[:, c * (q_chunk // HEAD_SIZE) + h, :] = rotate(
                block[:, h * HEAD_SIZE:(h + 1) * HEAD_SIZE] * scale
            )

    kv_copy.wait()
    inv_root = np.float32(1.0 / np.sqrt(np.float32(HEAD_SIZE)))
    column = lax.broadcasted_iota(jnp.int32, (heads, positions), 1)
    is_key = lax.rem(column, 2) == 0
    for r in range(local_rows):
        pairs = kv[r * positions:(r + 1) * positions, :]
        rquery = q_s[r].astype(jnp.bfloat16)
        scores = (
            lax.dot_general(
                rquery, pairs, (((1,), (1,)), ((), ())), preferred_element_type=jnp.float32
            )
            * inv_root
        )
        valid = jnp.logical_and(is_key, column < 2 * lens[r // here, r % here])
        scores = jnp.where(valid, scores, -1e30)
        new_score = (
            jnp.sum(rquery.astype(jnp.float32) * rkey[r:r + 1, :], axis=1, keepdims=True)
            * inv_root
        )
        top = jnp.maximum(jnp.max(scores, axis=1, keepdims=True), new_score)
        weights = jnp.exp(scores - top)
        new_weight = jnp.exp(new_score - top)
        total = jnp.sum(weights, axis=1, keepdims=True) + new_weight
        moved = pltpu.roll(weights, 1, 1).astype(jnp.bfloat16)
        mixed = jnp.dot(moved, pairs, preferred_element_type=jnp.float32)
        o_s[r] = (mixed + new_weight * value_new[r:r + 1, :]) / total

    for h in range(heads):
        att_send[:, h * HEAD_SIZE:(h + 1) * HEAD_SIZE] = o_s[:, h, :].astype(jnp.bfloat16)

    def spread(d):
        target = lax.rem(me + d, n)
        return pltpu.make_async_remote_copy(
            src_ref=att_send, dst_ref=att_recv.at[me],
            send_sem=as_sem.at[d], recv_sem=ar_sem.at[d],
            device_id={"gx": target}, device_id_type=MESH,
        )

    def gathered(d):
        source = lax.rem(me - d + n, n)
        return pltpu.make_async_remote_copy(
            src_ref=att_send, dst_ref=att_recv.at[source],
            send_sem=as_sem.at[d], recv_sem=ar_sem.at[d],
            device_id={"gx": source}, device_id_type=MESH,
        )

    each(lambda d: spread(d).start())
    att_recv[me] = att_send[...]
    each(lambda d: gathered(d).wait_recv())
    for j in range(n):
        block = att_recv[j].astype(jnp.float32)
        for b in range(batches):
            x_s[b * rows + j * here:b * rows + (j + 1) * here, :] = block[
                b * here:(b + 1) * here, :
            ]
    normed_att = x_s[...].astype(jnp.bfloat16)

    def cols_of(c):
        return pl.ds(pl.multiple_of(c * o_chunk, o_chunk), o_chunk)

    def halve(c):
        cols = cols_of(c)
        return pltpu.make_async_remote_copy(
            src_ref=ybuf.at[1 - bit, :, cols], dst_ref=r1.at[:, cols],
            send_sem=d_send.at[c], recv_sem=d_recv.at[c],
            device_id={"gy": across(0)}, device_id_type=MESH,
        )

    def exchange(c, level):
        cols = cols_of(c)
        return pltpu.make_async_remote_copy(
            src_ref=s2.at[level - 1, :, cols], dst_ref=r2.at[level - 1, :, cols],
            send_sem=e_send.at[level - 1, c], recv_sem=e_recv.at[level - 1, c],
            device_id={"gy": across(level)}, device_id_type=MESH,
        )

    def share(c):
        cols = cols_of(c)
        return pltpu.make_async_remote_copy(
            src_ref=out.at[bit, :, cols], dst_ref=out.at[bit, :, cols],
            send_sem=f_send.at[c], recv_sem=f_recv.at[c],
            device_id={"gy": across(0)}, device_id_type=MESH,
        )

    def shared(c):
        cols = cols_of(c)
        return pltpu.make_async_remote_copy(
            src_ref=out.at[1 - bit, :, cols], dst_ref=out.at[1 - bit, :, cols],
            send_sem=f_send.at[c], recv_sem=f_recv.at[c],
            device_id={"gy": across(0)}, device_id_type=MESH,
        )

    def multiply(c):
        cols = cols_of(c)
        wo_copy(c).wait()
        y = jnp.dot(normed_att, wo[:, cols], preferred_element_type=jnp.float32)
        ybuf[:, :, cols] = y.reshape(2, half, o_chunk)
        halve(c).start()

    def combine(c):
        cols = cols_of(c)
        halve(c).wait_recv()
        s2[0, :, cols] = ybuf[bit, :, cols] + r1[:, cols]
        exchange(c, 1).start()

    def between(c, level):
        cols = cols_of(c)
        exchange(c, level).wait_recv()
        s2[level, :, cols] = s2[level - 1, :, cols] + r2[level - 1, :, cols]
        exchange(c, level + 1).start()

    def close(c):
        cols = cols_of(c)
        last = bits - 1
        exchange(c, last).wait_recv()
        total = s2[last - 1, :, cols] + r2[last - 1, :, cols]
        out[bit, :, cols] = (tok[bit, :, cols].astype(jnp.float32) + total).astype(jnp.bfloat16)
        share(c).start()

    stages = [(0, multiply), (2, combine)]
    for level in range(1, bits - 1):
        stages.append((stages[-1][0] + 4, functools.partial(between, level=level)))
    stages.append((stages[-1][0] + 4, close))

    def tick(t, carry):
        for lag, stage in stages:
            @pl.when(jnp.logical_and(t >= lag, t < no + lag))
            def _(lag=lag, stage=stage):
                stage(t - lag)
        return carry

    lax.fori_loop(0, no + stages[-1][0], tick, 0)

    def drain(c, carry):
        halve(c).wait_send()
        for level in range(1, bits):
            exchange(c, level).wait_send()
        share(c).wait_send()
        shared(c).wait_recv()
        return carry

    lax.fori_loop(0, no, drain, 0)
    each(lambda d: spread(d).wait_send())
    each(lambda d: shift(nq, d, q_width, side).wait_send())
    for c in range(nq):
        each(lambda d: shift(c, d, c * q_chunk, q_chunk).wait_send())


def local(n, ny, tokens, lengths, norm_gain, w_query, key_value_weight, w_out, cache):
    batches, rows, depth = tokens.shape
    here = rows // n
    local_rows = batches * here
    q_width = w_query.shape[1]
    kv_heads = key_value_weight.shape[1]
    kv_width = kv_heads * key_value_weight.shape[2]
    assert kv_heads == 1 and ny >= 4 and ny & (ny - 1) == 0 and batches == 2
    heads = q_width // HEAD_SIZE
    out_width = w_out.shape[1]
    q_chunk = 512 if n <= 8 else q_width
    o_chunk = min(512, out_width)
    nq, no = q_width // q_chunk, out_width // o_chunk
    bits = ny.bit_length() - 1
    half = batches * rows // 2
    wide = q_width + kv_width + HEAD_SIZE
    freq = np.float32(ROPE_BASE) ** (
        -2.0 * np.arange(HEAD_SIZE // 2, dtype=np.float32) / HEAD_SIZE
    )
    freq = np.concatenate([freq, freq]).astype(np.float32)[None, :]
    pairs = cache.reshape(local_rows * cache.shape[2] * 2, HEAD_SIZE)
    any_space = pl.BlockSpec(memory_space=pl.ANY)
    f32, bf16 = jnp.float32, jnp.bfloat16
    dma = pltpu.SemaphoreType.DMA
    return pl.pallas_call(
        functools.partial(kernel, n, ny, q_chunk, o_chunk),
        out_shape=jax.ShapeDtypeStruct(tokens.shape, bf16),
        in_specs=[pl.BlockSpec(memory_space=pltpu.SMEM)] + [any_space] * 7,
        out_specs=pl.BlockSpec(memory_space=pltpu.VMEM),
        scratch_shapes=[
            pltpu.VMEM(tokens.shape, bf16),
            pltpu.VMEM((1, depth), f32),
            pltpu.VMEM((1, HEAD_SIZE), f32),
            pltpu.VMEM(w_query.shape, bf16),
            pltpu.VMEM((depth, kv_width), bf16),
            pltpu.VMEM(w_out.shape, bf16),
            pltpu.VMEM(pairs.shape, bf16),
            pltpu.VMEM((batches * rows, depth), bf16),
            pltpu.VMEM((n, local_rows, wide), f32),
            pltpu.VMEM((n, local_rows, wide), f32),
            pltpu.VMEM((local_rows, heads, HEAD_SIZE), f32),
            pltpu.VMEM((local_rows, heads, HEAD_SIZE), f32),
            pltpu.VMEM((local_rows, q_width), bf16),
            pltpu.VMEM((n, local_rows, q_width), bf16),
            pltpu.VMEM((batches * rows, q_width), f32),
            pltpu.VMEM((2, half, out_width), f32),
            pltpu.VMEM((half, out_width), f32),
            pltpu.VMEM((bits - 1, half, out_width), f32),
            pltpu.VMEM((bits - 1, half, out_width), f32),
            dma((3,)), dma((nq,)), dma, dma((no,)), dma,
            dma((nq + 1, n)), dma((nq + 1, n)), dma((n,)), dma((n,)),
            dma((no,)), dma((no,)), dma((bits - 1, no)), dma((bits - 1, no)),
            dma((no,)), dma((no,)),
        ],
        compiler_params=pltpu.CompilerParams(
            collective_id=0, has_side_effects=True, vmem_limit_bytes=60 * 1024 * 1024
        ),
    )(
        lengths, tokens, norm_gain.astype(f32).reshape(1, depth), jnp.asarray(freq),
        w_query, key_value_weight.reshape(depth, kv_width), w_out, pairs,
    )


def solution(mesh):
    placed = (
        P(None, "groups", "gx"),
        P(None, ("groups", "gx")),
        P("gx"),
        P("gx", "gy"),
        P("gx", "gy", None),
        P("gy", "gx"),
        P(None, ("groups", "gx"), None, "gy", None, None),
    )
    return jax.shard_map(
        functools.partial(local, mesh.shape["gx"], mesh.shape["gy"]),
        mesh=mesh, in_specs=placed, out_specs=P(None, "groups", "gx"), check_vma=False,
    )
```

time: 122 us -> 38.1 us (0.31)
  waiting for transfers between devices: 39.5 us -> 0 us
  Pallas kernels: 0 us -> 35 us
  blocking collectives: 33.9 us -> 0 us
  matrix products: 22 us -> 0 us
  between operations: 14.2 us -> 0.01 us
  local copies, waits for them, and re-layouts: 8.61 us -> 1.57 us
  other arithmetic: 3.71 us -> 1.3 us
    pallas_call x0 -> x1, Pallas kernels: none -> 35 us  [local(): pl.pallas_call(functools.partial(kernel, n, ny, q_chunk, o_chunk), out_sh...]
    psum x1 -> x0, waiting for transfers between devices: 32.2 us -> none  [local(): summed_heads = lax.psum(projected, 'gy')]
    dot_general x5 -> x0, matrix products: 22 us -> none  [the longest x1 8.81 us: local(): jnp.einsum('mrd,dc->mrc', normed, w_query, preferred_element_type=jnp.flo...]
    unnamed x1 -> x0, blocking collectives: 20.8 us -> none
    all_gather x1 -> x0, blocking collectives: 13.1 us -> none  [local(): lax.all_gather(attended, 'gx', axis=1, tiled=True)]
    unnamed x3 -> x0, waiting for transfers between devices: 7.38 us -> none
    slice x1 -> x0, local copies, waits for them, and re-layouts: 6.95 us -> none  [attend(): keys = cache[:, :, :, :, 0, :]]
    convert_element_type x3 -> x0, other arithmetic: 2.48 us -> none  [the longest x1 1.63 us: local(): return (x_full + summed_heads).astype(jnp.bfloat16)]
  transfers between devices with their start and end apart: 2 -> 0, of which waited for: 2 -> 0; matrix products, arithmetic and copies ran while one was open for 7% -> 0% of each run, Pallas kernels for 0% -> 0%
where the time goes in v1:
time: 38.1 us; the launch traced here: 37.9 us
  Pallas kernels  35 us (92%)
  local copies, waits for them, and re-layouts  1.57 us (4%)
  other arithmetic  1.3 us (3%)
    pallas_call x1, Pallas kernels, local(): pl.pallas_call(functools.partial(kernel, n, ny, q_chunk, o_chunk), out_sh...  35 us
    unnamed x1, local copies, waits for them, and re-layouts  1.57 us
    reshape x1, other arithmetic, local(): norm_gain.astype(f32).reshape(1, depth)  1.3 us

profile of v1, /device:TPU:0, one launch (start us, length us, event | category | flops | bytes accessed | tf_op | source)
XLA Modules:
  0.0 37.9 jit_solution(6478683549786650980)
XLA Ops:
  0.0 1.3 %reshape.15 = f32[4096]{0:T(1024)} convert(bf16[4096]{0:T(1024)(128)(2,1)} %param.10) | non-fusion elementwise | flops 4096 | bytes 24576 | tf_op jit(solution)/shard_map/reshape | solution.py:396
  1.3 35.0 %shard_map.82 = bf16[2,8,4096]{2,1,0:T(8,128)(2,1)} custom-call(s32[2,2]{1,0:T(2,128)} %lens.1, bf16[2,8,4096]{2,1,0:T(8,128)(2,1)} %tok_hbm.1, f32[1,4096]{1,0:T(1,128)} %bitcast.5, f32[1,128]{1,0:T(1,128)} %constant.2.clone.freq_hbm, bf16[4096,2048]{1,0:T(8,128)(2,1)} %wq_hbm.1, bf16[4096,256]{1,0:T(8,128)(2,1)} %bitcast.3, bf16[2048,4096]{1,0:T(8,128)(2,1)} %wo_hbm.1, ...), custom_call_target="tpu_custom_call" | custom-call | tf_op jit(solution)/shard_map/pallas_call | solution.py:362
  36.3 1.6 %copy.10 = bf16[2,8,4096]{2,1,0:T(8,128)(2,1)} copy(bf16[2,8,4096]{2,1,0:T(8,128)(2,1)} %shard_map.82) | data formatting | bytes 262144

commit v2 on v1

--- a/solution.py
+++ b/solution.py
@@ -21,7 +21,7 @@
     tok, gain, freq, wq, wk, wo, kv, normed,
     send, recv, q_s, o_s, att_send, att_recv, x_s, ybuf, r1, s2, r2,
     small_sem, wq_sem, wk_sem, wo_sem, kv_sem,
-    qs_sem, qr_sem, as_sem, ar_sem, d_send, d_recv, e_send, e_recv, f_send, f_recv,
+    qs_sem, qr_sem, as_sem, ar_sem, e_send, e_recv,
 ):
     batches, rows, depth = tok.shape
     here = rows // n
@@ -34,10 +34,8 @@
     no = out_width // o_chunk
     local_rows = batches * here
     positions = kv.shape[0] // local_rows
-    half = total_rows // 2
     me = lax.axis_index("gx")
     my = lax.axis_index("gy")
-    bit = lax.rem(my, 2)
 
     smalls = [
         pltpu.make_async_copy(tok_hbm, tok, small_sem.at[0]),
@@ -60,9 +58,6 @@
     kv_copy = pltpu.make_async_copy(kv_hbm, kv, kv_sem)
     for c in range(nq):
         wq_copy(c).start()
-    kv_copy.start()
-    for c in range(no):
-        wo_copy(c).start()
 
     barrier = pltpu.get_barrier_semaphore()
 
@@ -85,7 +80,9 @@
     for copy in smalls:
         copy.wait()
     x = tok[...].astype(jnp.float32).reshape(total_rows, depth)
-    normed[...] = (x * gain[...]).astype(jnp.bfloat16)
+    for k in range(depth // HEAD_SIZE):
+        cols = slice(k * HEAD_SIZE, (k + 1) * HEAD_SIZE)
+        normed[:, cols] = (x[:, cols] * gain[k:k + 1, :].astype(jnp.float32)).astype(jnp.bfloat16)
     squares = jnp.broadcast_to(jnp.sum(x * x, axis=1, keepdims=True), (total_rows, HEAD_SIZE))
 
     def put(part, start):
@@ -137,6 +134,13 @@
     def project(c, carry):
         start = pl.multiple_of(c * q_chunk, q_chunk)
         wq_copy(c).wait()
+
+        @pl.when(c == max(nq - 2, 0))
+        def _():
+            kv_copy.start()
+            for o in range(no):
+                wo_copy(o).start()
+
         put(
             jnp.dot(
                 normed[...], wq[:, pl.ds(start, q_chunk)], preferred_element_type=jnp.float32
@@ -247,69 +251,43 @@
     def cols_of(c):
         return pl.ds(pl.multiple_of(c * o_chunk, o_chunk), o_chunk)
 
-    def halve(c):
+    def exchange(c, k):
         cols = cols_of(c)
         return pltpu.make_async_remote_copy(
-            src_ref=ybuf.at[1 - bit, :, cols], dst_ref=r1.at[:, cols],
-            send_sem=d_send.at[c], recv_sem=d_recv.at[c],
-            device_id={"gy": across(0)}, device_id_type=MESH,
-        )
-
-    def exchange(c, level):
-        cols = cols_of(c)
-        return pltpu.make_async_remote_copy(
-            src_ref=s2.at[level - 1, :, cols], dst_ref=r2.at[level - 1, :, cols],
-            send_sem=e_send.at[level - 1, c], recv_sem=e_recv.at[level - 1, c],
-            device_id={"gy": across(level)}, device_id_type=MESH,
-        )
-
-    def share(c):
-        cols = cols_of(c)
-        return pltpu.make_async_remote_copy(
-            src_ref=out.at[bit, :, cols], dst_ref=out.at[bit, :, cols],
-            send_sem=f_send.at[c], recv_sem=f_recv.at[c],
-            device_id={"gy": across(0)}, device_id_type=MESH,
-        )
-
-    def shared(c):
-        cols = cols_of(c)
-        return pltpu.make_async_remote_copy(
-            src_ref=out.at[1 - bit, :, cols], dst_ref=out.at[1 - bit, :, cols],
-            send_sem=f_send.at[c], recv_sem=f_recv.at[c],
-            device_id={"gy": across(0)}, device_id_type=MESH,
+            src_ref=ybuf.at[:, cols] if k == 0 else s2.at[k - 1, :, cols],
+            dst_ref=r1.at[:, cols] if k == 0 else r2.at[k - 1, :, cols],
+            send_sem=e_send.at[k, c], recv_sem=e_recv.at[k, c],
+            device_id={"gy": across(bits - 1 - k)}, device_id_type=MESH,
         )
 
     def multiply(c):
         cols = cols_of(c)
         wo_copy(c).wait()
-        y = jnp.dot(normed_att, wo[:, cols], preferred_element_type=jnp.float32)
-        ybuf[:, :, cols] = y.reshape(2, half, o_chunk)
-        halve(c).start()
-
-    def combine(c):
+        ybuf[:, cols] = jnp.dot(
+            normed_att, wo[:, cols], preferred_element_type=jnp.float32
+        ).astype(jnp.bfloat16)
+        exchange(c, 0).start()
+
+    def so_far(c, k):
         cols = cols_of(c)
-        halve(c).wait_recv()
-        s2[0, :, cols] = ybuf[bit, :, cols] + r1[:, cols]
-        exchange(c, 1).start()
-
-    def between(c, level):
-        cols = cols_of(c)
-        exchange(c, level).wait_recv()
-        s2[level, :, cols] = s2[level - 1, :, cols] + r2[level - 1, :, cols]
-        exchange(c, level + 1).start()
+        exchange(c, k).wait_recv()
+        if k == 0:
+            return ybuf[:, cols].astype(jnp.float32) + r1[:, cols].astype(jnp.float32)
+        return s2[k - 1, :, cols] + r2[k - 1, :, cols]
+
+    def combine(c, k):
+        s2[k, :, cols_of(c)] = so_far(c, k)
+        exchange(c, k + 1).start()
 
     def close(c):
         cols = cols_of(c)
-        last = bits - 1
-        exchange(c, last).wait_recv()
-        total = s2[last - 1, :, cols] + r2[last - 1, :, cols]
-        out[bit, :, cols] = (tok[bit, :, cols].astype(jnp.float32) + total).astype(jnp.bfloat16)
-        share(c).start()
-
-    stages = [(0, multiply), (2, combine)]
-    for level in range(1, bits - 1):
-        stages.append((stages[-1][0] + 4, functools.partial(between, level=level)))
-    stages.append((stages[-1][0] + 4, close))
+        total = so_far(c, bits - 1).reshape(batches, rows, o_chunk)
+        out[:, :, cols] = (tok[:, :, cols].astype(jnp.float32) + total).astype(jnp.bfloat16)
+
+    stages = [(0, multiply)]
+    for k in range(bits - 1):
+        stages.append((stages[-1][0] + 3, functools.partial(combine, k=k)))
+    stages.append((stages[-1][0] + 1, close))
 
     def tick(t, carry):
         for lag, stage in stages:
@@ -321,11 +299,8 @@
     lax.fori_loop(0, no + stages[-1][0], tick, 0)
 
     def drain(c, carry):
-        halve(c).wait_send()
-        for level in range(1, bits):
-            exchange(c, level).wait_send()
-        share(c).wait_send()
-        shared(c).wait_recv()
+        for k in range(bits):
+            exchange(c, k).wait_send()
         return carry
 
     lax.fori_loop(0, no, drain, 0)
@@ -342,31 +317,30 @@
     q_width = w_query.shape[1]
     kv_heads = key_value_weight.shape[1]
     kv_width = kv_heads * key_value_weight.shape[2]
-    assert kv_heads == 1 and ny >= 4 and ny & (ny - 1) == 0 and batches == 2
+    assert kv_heads == 1 and ny >= 4 and ny & (ny - 1) == 0
     heads = q_width // HEAD_SIZE
     out_width = w_out.shape[1]
-    q_chunk = 512 if n <= 8 else q_width
-    o_chunk = min(512, out_width)
+    q_chunk = 1024 if n <= 8 else q_width
+    o_chunk = min(1024, out_width)
     nq, no = q_width // q_chunk, out_width // o_chunk
     bits = ny.bit_length() - 1
-    half = batches * rows // 2
     wide = q_width + kv_width + HEAD_SIZE
     freq = np.float32(ROPE_BASE) ** (
         -2.0 * np.arange(HEAD_SIZE // 2, dtype=np.float32) / HEAD_SIZE
     )
     freq = np.concatenate([freq, freq]).astype(np.float32)[None, :]
     pairs = cache.reshape(local_rows * cache.shape[2] * 2, HEAD_SIZE)
-    any_space = pl.BlockSpec(memory_space=pl.ANY)
+    any_space = pl.BlockSpec(memory_space=pltpu.HBM)
     f32, bf16 = jnp.float32, jnp.bfloat16
     dma = pltpu.SemaphoreType.DMA
     return pl.pallas_call(
         functools.partial(kernel, n, ny, q_chunk, o_chunk),
-        out_shape=jax.ShapeDtypeStruct(tokens.shape, bf16),
+        out_shape=pltpu.VMEM(tokens.shape, bf16),
         in_specs=[pl.BlockSpec(memory_space=pltpu.SMEM)] + [any_space] * 7,
         out_specs=pl.BlockSpec(memory_space=pltpu.VMEM),
         scratch_shapes=[
             pltpu.VMEM(tokens.shape, bf16),
-            pltpu.VMEM((1, depth), f32),
+            pltpu.VMEM((depth // HEAD_SIZE, HEAD_SIZE), bf16),
             pltpu.VMEM((1, HEAD_SIZE), f32),
             pltpu.VMEM(w_query.shape, bf16),
             pltpu.VMEM((depth, kv_width), bf16),
@@ -380,20 +354,19 @@
             pltpu.VMEM((local_rows, q_width), bf16),
             pltpu.VMEM((n, local_rows, q_width), bf16),
             pltpu.VMEM((batches * rows, q_width), f32),
-            pltpu.VMEM((2, half, out_width), f32),
-            pltpu.VMEM((half, out_width), f32),
-            pltpu.VMEM((bits - 1, half, out_width), f32),
-            pltpu.VMEM((bits - 1, half, out_width), f32),
+            pltpu.VMEM((batches * rows, out_width), bf16),
+            pltpu.VMEM((batches * rows, out_width), bf16),
+            pltpu.VMEM((bits - 1, batches * rows, out_width), f32),
+            pltpu.VMEM((bits - 1, batches * rows, out_width), f32),
             dma((3,)), dma((nq,)), dma, dma((no,)), dma,
             dma((nq + 1, n)), dma((nq + 1, n)), dma((n,)), dma((n,)),
-            dma((no,)), dma((no,)), dma((bits - 1, no)), dma((bits - 1, no)),
-            dma((no,)), dma((no,)),
+            dma((bits, no)), dma((bits, no)),
         ],
         compiler_params=pltpu.CompilerParams(
-            collective_id=0, has_side_effects=True, vmem_limit_bytes=60 * 1024 * 1024
+            collective_id=0, has_side_effects=True, vmem_limit_bytes=67043328 - 2 * tokens.size
         ),
     )(
-        lengths, tokens, norm_gain.astype(f32).reshape(1, depth), jnp.asarray(freq),
+        lengths, tokens, norm_gain.reshape(depth // HEAD_SIZE, HEAD_SIZE), jnp.asarray(freq),
         w_query, key_value_weight.reshape(depth, kv_width), w_out, pairs,
     )
 

time: 38.1 us -> 28.5 us (0.75)
  Pallas kernels: 35 us -> 27.7 us
  other arithmetic: 1.3 us -> 0 us
  local copies, waits for them, and re-layouts: 1.57 us -> 0.66 us
    pallas_call x1, Pallas kernels: 35 us -> 27.7 us  [local(): pl.pallas_call(functools.partial(kernel, n, ny, q_chunk, o_chunk), out_sh...]
    reshape x1 -> x0, other arithmetic: 1.3 us -> none  [local(): norm_gain.astype(f32).reshape(1, depth)]
    unnamed x1, local copies, waits for them, and re-layouts: 1.57 us -> 0.66 us
where the time goes in v2:
time: 28.5 us; the launch traced here: 28.4 us
  Pallas kernels  27.7 us (97%)
  local copies, waits for them, and re-layouts  0.66 us (2%)
    pallas_call x1, Pallas kernels, local(): pl.pallas_call(functools.partial(kernel, n, ny, q_chunk, o_chunk), out_sh...  27.7 us
    unnamed x1, local copies, waits for them, and re-layouts  0.66 us

profile of v2, /device:TPU:0, one launch (start us, length us, event | category | flops | bytes accessed | tf_op | source)
XLA Modules:
  0.0 28.4 jit_solution(1996853774373217445)
XLA Ops:
  0.0 27.7 %shard_map.82 = bf16[2,8,4096]{2,1,0:T(8,128)(2,1)S(1)} custom-call(s32[2,2]{1,0:T(2,128)} %lens.1, bf16[2,8,4096]{2,1,0:T(8,128)(2,1)} %tok_hbm.1, bf16[32,128]{1,0:T(8,128)(2,1)} %bitcast.5, f32[1,128]{1,0:T(1,128)} %constant.2.clone.freq_hbm, bf16[4096,2048]{1,0:T(8,128)(2,1)} %wq_hbm.1, bf16[4096,256]{1,0:T(8,128)(2,1)} %bitcast.3, ...), custom_call_target="tpu_custom_call" | custom-call | tf_op jit(solution)/shard_map/pallas_call | solution.py:336
  27.7 0.7 %copy.10 = bf16[2,8,4096]{2,1,0:T(8,128)(2,1)} copy(bf16[2,8,4096]{2,1,0:T(8,128)(2,1)S(1)} %shard_map.82) | data formatting | bytes 262144
